TPU v7x, 32 devices: a whole 2x2x4 slice. The times are simulated.
32 devices in a mesh: rows: 8 (over y, x, core), width: 4 (over z).
Axes of the slice: x: 2, y: 2, z: 4, core: 2. Of those that a mesh axis runs over, the one named last changes fastest.
Arguments:
- one_query: float32 [7168, 7168], P('rows', 'width'), may hold values from -0.09375 to 0.09375
- other_query: float32 [7168, 7168], P('rows', 'width'), may hold values from -0.0625 to 0.0625
- one_key: float32 [7168, 1024], P('rows', 'width'), may hold values from -0.09375 to 0.09375
- other_key: float32 [7168, 1024], P('rows', 'width'), may hold values from -0.0625 to 0.0625
- one_value: float32 [7168, 1024], P('rows', 'width'), may hold values from -0.09375 to 0.09375
- other_value: float32 [7168, 1024], P('rows', 'width'), may hold values from -0.0625 to 0.0625
- mix_share: float32 [7168], P('rows'), may hold values from 0.2 to 0.8
- norm_train: float32 [7168], P(('rows', 'width')), may hold values from 0.25 to 1.75
- norm_step: float32 [7168], P(('rows', 'width')), may hold values from -0.3 to 0.3
Outputs:
- final_query: bfloat16 [7168, 7168], P(None, 'width')
- final_key: bfloat16 [7168, 1024], P(None, 'width')
- final_value: bfloat16 [7168, 1024], P(None, 'width')
- column_query: float32 [7168], P('width')
- column_key: float32 [1024], P('width')
- column_value: float32 [1024], P('width')
- serve_norm: bfloat16 [7168], replicated
All inputs are finite; a program needn't handle non-finite values.
Results may differ from a plain program's by a relative error of at most 0.001.
Values may be sent and summed in bfloat16 or wider, within the bound.
A program may use at most 128 MiB of HBM per device.

v0:
```python
import jax
import jax.numpy as jnp
from jax import lax
from jax.sharding import PartitionSpec as P


def shards(
    one_query,
    other_query,
    one_key,
    other_key,
    one_value,
    other_value,
    mix_share,
    norm_train,
    norm_step,
):
    result_query = mix_share[:, None] * one_query + (1.0 - mix_share[:, None]) * other_query
    result_key = mix_share[:, None] * one_key + (1.0 - mix_share[:, None]) * other_key
    result_value = mix_share[:, None] * one_value + (1.0 - mix_share[:, None]) * other_value
    total_query, total_key, total_value = lax.psum(
        (
            jnp.sum(result_query * result_query, axis=0),
            jnp.sum(result_key * result_key, axis=0),
            jnp.sum(result_value * result_value, axis=0),
        ),
        "rows",
    )
    column_query = jnp.sqrt(total_query)
    column_key = jnp.sqrt(total_key)
    column_value = jnp.sqrt(total_value)
    narrow_query, narrow_key, narrow_value = (
        (result_query / column_query).astype(jnp.bfloat16),
        (result_key / column_key).astype(jnp.bfloat16),
        (result_value / column_value).astype(jnp.bfloat16),
    )
    final_query, final_key, final_value = (
        lax.all_gather(narrow_query, "rows", axis=0, tiled=True),
        lax.all_gather(narrow_key, "rows", axis=0, tiled=True),
        lax.all_gather(narrow_value, "rows", axis=0, tiled=True),
    )
    serve_norm = lax.all_gather(
        (norm_train + norm_step).astype(jnp.bfloat16), ("rows", "width"), axis=0, tiled=True
    )
    return (final_query, final_key, final_value, column_query, column_key, column_value, serve_norm)


def solution(mesh):
    in_specs = (
        P("rows", "width"),
        P("rows", "width"),
        P("rows", "width"),
        P("rows", "width"),
        P("rows", "width"),
        P("rows", "width"),
        P("rows"),
        P(("rows", "width")),
        P(("rows", "width")),
    )
    out_specs = (
        P(None, "width"),
        P(None, "width"),
        P(None, "width"),
        P("width"),
        P("width"),
        P("width"),
        P(),
    )
    return jax.shard_map(shards, mesh=mesh, in_specs=in_specs, out_specs=out_specs, check_vma=False)
```

profile of v0, /device:TPU:0, one launch (start us, length us, event | category | flops | bytes accessed | tf_op | source)
XLA Modules:
  0.0 276.2 jit_solution(12570724530441781290)
XLA Ops:
  7.2 0.0 all-gather.6.cloned.1.call-start
  7.2 0.7 broadcast_subtract_fusion
  7.9 0.0 copy-start.6
  7.9 5.5 %multiply_reduce_fusion = f32[1792]{0:T(1024)S(1)} fusion(f32[896,1792]{1,0:T(8,128)} %param.10, f32[896]{0:T(1024)S(1)} %broadcast_subtract_fusion, f32[896,1792]{1,0:T(8,128)} %param.9, f32[896]{0:T(1024)} %param.15), kind=kLoop, calls=%fused_computation.1 | loop fusion | flops 8026368 | bytes 12859392 | tf_op jit(solution)/shard_map/reduce_sum | solution.py:23
  13.5 0.0 copy-done.2
  13.5 0.0 copy-done.3
  13.5 0.0 copy-done.4
  13.5 0.1 copy-done.5
  13.6 0.0 copy-done.6
  13.6 0.4 multiply_reduce_fusion.1
  14.0 25.5 %all-reduce.1 = (f32[1792]{0:T(1024)S(1)}, f32[256]{0:T(256)S(1)}, f32[256]{0:T(256)S(1)}) all-reduce(f32[1792]{0:T(1024)S(1)} %multiply_reduce_fusion, f32[256]{0:T(256)S(1)} %get-tuple-element.8, f32[256]{0:T(256)S(1)} %get-tuple-element.7), channel_id=1, replica_groups=mesh['rows'=8,'width'=4] {'rows'}, use_global_device_ids=true, to_apply=%region_1.0 | all-reduce | flops 2304 | bytes 18432 | tf_op jit(solution)/shard_map/psum | solution.py:21
  39.6 0.0 copy-start.9
  39.6 2.5 divide_convert_fusion.1
  42.1 0.0 all-gather.6.cloned.1.call-update
  42.1 0.0 all-gather.8.cloned.1.call-start
  42.1 0.7 all-gather.8.cloned.1.call-update
  42.8 0.0 all-gather.4.cloned.1.call-start
  42.9 0.0 copy-start.7
  42.9 0.0 copy-start.10
  42.9 0.0 copy-start.11
  42.9 7.1 %divide_convert_fusion = bf16[896,1792]{1,0:T(8,128)(2,1)} fusion(f32[1792]{0:T(1024)S(1)} %sqrt.9, f32[896,1792]{1,0:T(8,128)} %param.10, f32[896]{0:T(1024)S(1)} %broadcast_subtract_fusion, f32[896,1792]{1,0:T(8,128)} %param.9, f32[896]{0:T(1024)S(1)} %copy-done.6), kind=kLoop, calls=%fused_computation | loop fusion | flops 8028160 | bytes 16070656 | tf_op jit(solution)/shard_map/convert_element_type | solution.py:33
  50.0 0.0 copy-done.8
  50.0 0.0 copy-done.7
  50.0 0.0 all-gather.4.cloned.1.call-update
  50.1 0.2 dynamic-update-slice
  50.3 39.8 %all-reduce = bf16[7168]{0:T(1024)(128)(2,1)} all-reduce(bf16[7168]{0:T(1024)(128)(2,1)S(1)} %dynamic-update-slice), channel_id=1, replica_groups=mesh['rows'=8,'width'=4] {'rows','width'}, use_global_device_ids=true, to_apply=%add | all-reduce | flops 7168 | bytes 28672
  90.1 23.4 %all-gather.8.cloned.1.call-done = bf16[7168,256]{1,0:T(8,128)(2,1)} async-done(((bf16[896,256]{1,0:T(8,128)(2,1)}), bf16[7168,256]{1,0:T(8,128)(2,1)}) %all-gather.8.cloned.1.call-update) | async-done | bytes 3670032 | tf_op jit(solution)/shard_map/all_gather | solution.py:40
  113.5 129.9 %all-gather.4.cloned.1.call-done = bf16[7168,1792]{1,0:T(8,128)(2,1)} async-done(((bf16[896,1792]{1,0:T(8,128)(2,1)}), bf16[7168,1792]{1,0:T(8,128)(2,1)}) %all-gather.4.cloned.1.call-update) | async-done | bytes 25690128 | tf_op jit(solution)/shard_map/all_gather | solution.py:38
  243.4 21.0 %copy.20 = bf16[7168,1792]{1,0:T(8,128)(2,1)} copy(bf16[7168,1792]{1,0:T(8,128)(2,1)} %all-gather.4.cloned.1.call-done) | data formatting | bytes 51380224
  264.5 1.9 copy.21
  266.4 1.5 copy-done.1
  267.9 1.8 copy.22
  (17 shorter events, 0.0 us)
Async XLA Ops:
  7.2 83.0 %all-gather.6.cloned.1.call-start = ((), (), s32[]{:S(2)}) async-start(), calls=%async_computation.1 | async-start | bytes 4128768 | tf_op jit(solution)/shard_map/all_gather | solution.py:39
  7.9 5.6 %copy-start.2 = (f32[896,256]{1,0:T(8,128)S(1)}, f32[896,256]{1,0:T(8,128)}, u32[]{:S(2)}) copy-start(f32[896,256]{1,0:T(8,128)} %param.14) | copy-start | bytes 2752516
  7.9 5.6 %copy-start.3 = (f32[896,256]{1,0:T(8,128)S(1)}, f32[896,256]{1,0:T(8,128)}, u32[]{:S(2)}) copy-start(f32[896,256]{1,0:T(8,128)} %param.13) | copy-start | bytes 2752516
  7.9 5.6 %copy-start.4 = (f32[896,256]{1,0:T(8,128)S(1)}, f32[896,256]{1,0:T(8,128)}, u32[]{:S(2)}) copy-start(f32[896,256]{1,0:T(8,128)} %param.12) | copy-start | bytes 2752516
  7.9 5.7 %copy-start.5 = (f32[896,256]{1,0:T(8,128)S(1)}, f32[896,256]{1,0:T(8,128)}, u32[]{:S(2)}) copy-start(f32[896,256]{1,0:T(8,128)} %param.11) | copy-start | bytes 2752516
  7.9 5.7 %copy-start.6 = (f32[896]{0:T(1024)S(1)}, f32[896]{0:T(1024)}, u32[]{:S(2)}) copy-start(f32[896]{0:T(1024)} %param.15) | copy-start | bytes 10756
  39.6 10.4 %copy-start.8 = (f32[256]{0:T(256)}, f32[256]{0:T(256)S(1)}, u32[]{:S(2)}) copy-start(f32[256]{0:T(256)S(1)} %sqrt.11) | copy-start | bytes 3076
  39.6 10.4 %copy-start.9 = (f32[256]{0:T(256)}, f32[256]{0:T(256)S(1)}, u32[]{:S(2)}) copy-start(f32[256]{0:T(256)S(1)} %sqrt.10) | copy-start | bytes 3076
  42.1 71.5 %all-gather.8.cloned.1.call-start = ((), (), s32[]{:S(2)}) async-start(), calls=%async_computation.2 | async-start | bytes 4128768 | tf_op jit(solution)/shard_map/all_gather | solution.py:40
  42.8 200.6 %all-gather.4.cloned.1.call-start = ((), (), s32[]{:S(2)}) async-start(), calls=%async_computation | async-start | bytes 28901376 | tf_op jit(solution)/shard_map/all_gather | solution.py:38
  42.9 7.1 %copy-start.7 = (f32[1792]{0:T(1024)}, f32[1792]{0:T(1024)S(1)}, u32[]{:S(2)}) copy-start(f32[1792]{0:T(1024)S(1)} %sqrt.9) | copy-start | bytes 21508
  42.9 7.1 %copy-start.10 = (f32[224]{0:T(256)S(1)}, f32[224]{0:T(256)}, u32[]{:S(2)}) copy-start(f32[224]{0:T(256)} %param.16) | copy-start | bytes 2692
  42.9 7.1 %copy-start.11 = (f32[224]{0:T(256)S(1)}, f32[224]{0:T(256)}, u32[]{:S(2)}) copy-start(f32[224]{0:T(256)} %param.17) | copy-start | bytes 2692
  243.4 21.1 %copy-start = (bf16[7168,256]{1,0:T(8,128)(2,1)S(1)}, bf16[7168,256]{1,0:T(8,128)(2,1)}, u32[]{:S(2)}) copy-start(bf16[7168,256]{1,0:T(8,128)(2,1)} %all-gather.6.cloned.1.call-done) | copy-start | bytes 11010052
  264.5 3.4 %copy-start.1 = (bf16[7168,256]{1,0:T(8,128)(2,1)S(1)}, bf16[7168,256]{1,0:T(8,128)(2,1)}, u32[]{:S(2)}) copy-start(bf16[7168,256]{1,0:T(8,128)(2,1)} %all-gather.8.cloned.1.call-done) | copy-start | bytes 11010052
Sparse Core Ops, SparseCore 0:
  42.2 34.3 all-gather.5
  79.0 34.4 all-gather.7
  116.0 127.3 all-gather.3
where the time goes:
time: 277 us; the launch traced here: 276 us
  waiting for transfers between devices  154 us (56%)
  blocking collectives  65.4 us (24%)
  local copies, waits for them, and re-layouts  26.7 us (10%)
  other arithmetic  16.1 us (6%)
  between operations  13.9 us (5%)
    all_gather x1, waiting for transfers between devices, shards(): lax.all_gather(narrow_query, 'rows', axis=0, tiled=True)  130 us
    unnamed x1, blocking collectives  39.8 us
    unnamed x29, local copies, waits for them, and re-layouts  26.7 us
    psum x1, blocking collectives, shards(): lax.psum((jnp.sum(result_query * result_query, axis=0), jnp.sum(result_ke...  25.5 us
    all_gather x1, waiting for transfers between devices, shards(): lax.all_gather(narrow_value, 'rows', axis=0, tiled=True)  23.4 us
    convert_element_type x1, other arithmetic, shards(): (result_query / column_query).astype(jnp.bfloat16)  7.05 us
  transfers between devices with their start and end apart: 3, of which 2 were waited for; matrix products, arithmetic and copies ran while one was open for 3% of the time, Pallas kernels for 0%

commit v1 on v0

v1 whole, which is shorter than its diff:
```python
import jax
import jax.numpy as jnp
from jax import lax
from jax.experimental import pallas as pl
from jax.experimental.pallas import tpu as pltpu
from jax.sharding import PartitionSpec as P

MESH = pl.DeviceIdType.MESH
LANES = 128


def kernel(
    n_rows,
    n_width,
    share,
    norm_in,
    one_query,
    other_query,
    one_key,
    other_key,
    one_value,
    other_value,
    *refs,
):
    blocks = refs[: 2 + one_query.shape[1] // one_key.shape[1]]
    col_query, col_key, col_value, norm_all, first, second, part, in_sem = refs[len(blocks) :][:8]
    norm_send, norm_recv, slab_send, slab_recv, sum_send, sum_recv = refs[len(blocks) + 8 :][:6]
    ring_send, ring_recv, twin_send, twin_recv = refs[len(blocks) + 14 :]
    me = lax.axis_index("rows")
    lane = lax.axis_index("width")
    depth, wide = one_key.shape
    groups = [
        (one_key, other_key, blocks[0], col_key, 0),
        (one_value, other_value, blocks[1], col_value, 0),
    ] + [
        (one_query, other_query, blocks[2 + j], col_query, j * wide)
        for j in range(one_query.shape[1] // wide)
    ]
    tile = 64 if depth % 64 == 0 else 16
    half = depth // 2

    loads = []
    for g, (one, other, _, _, at) in enumerate(groups):
        a = pltpu.make_async_copy(one.at[:, pl.ds(at, wide)], first.at[g], in_sem.at[0, g])
        b = pltpu.make_async_copy(other.at[:, pl.ds(at, wide)], second.at[g], in_sem.at[1, g])
        a.start()
        b.start()
        loads.append((a, b))

    norm_all[me, lane] = norm_in[...]

    barrier = pltpu.get_barrier_semaphore()
    for d in range(1, n_rows):
        pl.semaphore_signal(
            barrier, inc=1, device_id={"rows": lax.rem(me + d, n_rows)}, device_id_type=MESH
        )
    for d in range(1, n_width):
        pl.semaphore_signal(
            barrier, inc=1, device_id={"width": lax.rem(lane + d, n_width)}, device_id_type=MESH
        )
    pl.semaphore_wait(barrier, n_rows + n_width - 2)

    norm_copies = []
    for d in range(1, n_width):
        copy = pltpu.make_async_remote_copy(
            src_ref=norm_all.at[me, lane],
            dst_ref=norm_all.at[me, lane],
            send_sem=norm_send.at[d],
            recv_sem=norm_recv.at[d],
            device_id={"width": lax.rem(lane + d, n_width)},
            device_id_type=MESH,
        )
        copy.start()
        norm_copies.append(copy)

    for g in range(len(groups)):
        loads[g][0].wait()
        loads[g][1].wait()

        def mix(i, acc):
            rows = pl.ds(pl.multiple_of(i * tile, tile), tile)
            s = share[rows, :]
            s = jnp.concatenate([s] * (wide // LANES), axis=1)
            r = s * first[g, rows, :] + (1.0 - s) * second[g, rows, :]
            first[g, rows, :] = r
            return acc + jnp.sum((r * r).reshape(tile // 8, 8, wide), axis=0)

        acc = lax.fori_loop(0, depth // tile, mix, jnp.zeros((8, wide), jnp.float32))
        part[me, g] = jnp.sum(acc, axis=0, keepdims=True)

    sum_copies = []
    for d in range(1, n_rows):
        copy = pltpu.make_async_remote_copy(
            src_ref=part.at[me],
            dst_ref=part.at[me],
            send_sem=sum_send.at[d],
            recv_sem=sum_recv.at[d],
            device_id={"rows": lax.rem(me + d, n_rows)},
            device_id_type=MESH,
        )
        copy.start()
        sum_copies.append(copy)

    for copy in norm_copies:
        copy.wait_recv()
    slab_copies = []
    for d in range(1, n_rows):
        copy = pltpu.make_async_remote_copy(
            src_ref=norm_all.at[me],
            dst_ref=norm_all.at[me],
            send_sem=slab_send.at[d],
            recv_sem=slab_recv.at[d],
            device_id={"rows": lax.rem(me + d, n_rows)},
            device_id_type=MESH,
        )
        copy.start()
        slab_copies.append(copy)

    for copy in sum_copies:
        copy.wait_recv()

    core = lax.rem(me, 2)
    chip = me // 2
    chips = n_rows // 2
    reach = chips // 2

    def fold(c):
        return jnp.where(c < reach, c, 3 * reach - 1 - c)

    place = fold(chip)

    def device_at(step):
        return fold(lax.rem(place + step + chips, chips)) * 2 + core

    twin = me + 1 - 2 * core
    ahead = (device_at(1), device_at(-1))
    waits = []

    def region(g, owner, way, hop):
        if hop < reach:
            rows = pl.ds(pl.multiple_of(owner * depth, half), depth)
        else:
            rows = pl.ds(pl.multiple_of(owner * depth + way * half, half), half)
        return blocks[g].at[rows, :]

    def ring_copy(g, owner, way, hop):
        ref = region(g, owner, way, hop)
        copy = pltpu.make_async_remote_copy(
            src_ref=ref,
            dst_ref=ref,
            send_sem=ring_send.at[way, hop - 1, g],
            recv_sem=ring_recv.at[way, hop - 1, g],
            device_id={"rows": ahead[way]},
            device_id_type=MESH,
        )
        copy.start()
        return copy

    def twin_copy(g, owner, way, hop, slot):
        ref = region(g, owner, way, hop)
        copy = pltpu.make_async_remote_copy(
            src_ref=ref,
            dst_ref=ref,
            send_sem=twin_send.at[slot, g],
            recv_sem=twin_recv.at[slot, g],
            device_id={"rows": twin},
            device_id_type=MESH,
        )
        copy.start()
        waits.append(copy)

    flying = {}
    for g, (_, _, out, col, at) in enumerate(groups):
        total = part[0, g]
        for p in range(1, n_rows):
            total = total + part[p, g]
        scale = jnp.sqrt(total)
        col[:, pl.ds(at, wide)] = scale
        inverse = 1.0 / scale

        def narrow(i, carry):
            rows = pl.ds(pl.multiple_of(i * tile, tile), tile)
            here = pl.ds(pl.multiple_of(me * depth + i * tile, tile), tile)
            out[here, :] = (first[g, rows, :] * inverse).astype(out.dtype)
            return carry

        lax.fori_loop(0, depth // tile, narrow, 0)
        for way in range(2):
            flying[way, 1, g] = ring_copy(g, me, way, 1)
        twin_copy(g, me, 0, 0, 0)

    for hop in range(1, reach + 1):
        for g in range(len(groups)):
            for way in range(2):
                copy = flying[way, hop, g]
                copy.wait_recv()
                owner = device_at(-hop if way == 0 else hop)
                if hop < reach:
                    flying[way, hop + 1, g] = ring_copy(g, owner, way, hop + 1)
                twin_copy(g, owner, way, hop, 1 + 2 * (hop - 1) + way)

    for copy in flying.values():
        copy.wait_send()
    for copy in waits:
        copy.wait()
    for copy in norm_copies + sum_copies:
        copy.wait_send()
    for copy in slab_copies:
        copy.wait()


def store(*refs):
    outs, sem = refs[-8:-1], refs[-1]
    blocks, small = refs[:-12], refs[-12:-8]
    wide = blocks[0].shape[1]
    pairs = [(blocks[0], outs[1]), (blocks[1], outs[2])] + list(zip(small, outs[3:]))
    for j, block in enumerate(blocks[2:]):
        pairs.append((block, outs[0].at[:, pl.ds(j * wide, wide)]))
    copies = [pltpu.make_async_copy(src, dst, sem.at[i]) for i, (src, dst) in enumerate(pairs)]
    for copy in copies:
        copy.start()
    for copy in copies:
        copy.wait()


def solution(mesh):
    n_rows, n_width = mesh.shape["rows"], mesh.shape["width"]

    def shards(
        one_query,
        other_query,
        one_key,
        other_key,
        one_value,
        other_value,
        mix_share,
        norm_train,
        norm_step,
    ):
        depth, wide = one_key.shape
        wide_query = one_query.shape[1]
        count = 2 + wide_query // wide
        piece = norm_train.shape[0]
        padded = -(-piece // LANES) * LANES
        share = jnp.broadcast_to(mix_share[:, None], (depth, LANES))
        norm = jnp.pad(norm_train + norm_step, (0, padded - piece)).reshape(1, padded)
        total = depth * n_rows
        reach = n_rows // 4
        hbm = pl.BlockSpec(memory_space=pltpu.HBM)
        vmem = pl.BlockSpec(memory_space=pltpu.VMEM)
        dma = pltpu.SemaphoreType.DMA
        out_shape = (pltpu.VMEM((total, wide), jnp.bfloat16),) * count + (
            pltpu.VMEM((1, wide_query), jnp.float32),
            pltpu.VMEM((1, wide), jnp.float32),
            pltpu.VMEM((1, wide), jnp.float32),
            pltpu.VMEM((n_rows, n_width, 1, padded), jnp.float32),
        )
        gathered = pl.pallas_call(
            lambda *refs: kernel(n_rows, n_width, *refs),
            out_shape=out_shape,
            in_specs=[vmem] * 2 + [hbm] * 6,
            out_specs=[vmem] * (count + 4),
            scratch_shapes=[
                pltpu.VMEM((count, depth, wide), jnp.float32),
                pltpu.VMEM((count, depth, wide), jnp.float32),
                pltpu.VMEM((n_rows, count, 1, wide), jnp.float32),
                dma((2, count)),
                dma((n_width,)),
                dma((n_width,)),
                dma((n_rows,)),
                dma((n_rows,)),
                dma((n_rows,)),
                dma((n_rows,)),
                dma((2, reach, count)),
                dma((2, reach, count)),
                dma((1 + 2 * reach, count)),
                dma((1 + 2 * reach, count)),
            ],
            compiler_params=pltpu.CompilerParams(
                collective_id=0, has_side_effects=True, vmem_limit_bytes=24 * 1024 * 1024
            ),
        )(share, norm, one_query, other_query, one_key, other_key, one_value, other_value)
        final_query, final_key, final_value, col_query, col_key, col_value, norm_all = pl.pallas_call(
            store,
            out_shape=(
                jax.ShapeDtypeStruct((total, wide_query), jnp.bfloat16),
                jax.ShapeDtypeStruct((total, wide), jnp.bfloat16),
                jax.ShapeDtypeStruct((total, wide), jnp.bfloat16),
            )
            + tuple(jax.ShapeDtypeStruct(o.shape, o.dtype) for o in out_shape[count:]),
            in_specs=[vmem] * (count + 4),
            out_specs=[hbm] * 7,
            scratch_shapes=[dma((count + 4,))],
            compiler_params=pltpu.CompilerParams(vmem_limit_bytes=1024 * 1024),
        )(*gathered)
        serve_norm = norm_all[..., 0, :piece].astype(jnp.bfloat16).reshape(-1)
        return (
            final_query,
            final_key,
            final_value,
            col_query.reshape(-1),
            col_key.reshape(-1),
            col_value.reshape(-1),
            serve_norm,
        )

    wide_spec = P("rows", "width")
    in_specs = (wide_spec,) * 6 + (P("rows"), P(("rows", "width")), P(("rows", "width")))
    out_specs = (P(None, "width"),) * 3 + (P("width"),) * 3 + (P(),)
    return jax.shard_map(shards, mesh=mesh, in_specs=in_specs, out_specs=out_specs, check_vma=False)
```

time: 277 us -> 171 us (0.62)
  Pallas kernels: 0 us -> 162 us
  waiting for transfers between devices: 154 us -> 0 us
  blocking collectives: 65.4 us -> 0 us
  local copies, waits for them, and re-layouts: 26.7 us -> 6.87 us
  other arithmetic: 16.1 us -> 1.32 us
  between operations: 13.9 us -> 0.66 us
    pallas_call x0 -> x2, Pallas kernels: none -> 162 us  [the longest x1 151 us: shards(): pl.pallas_call(lambda *refs: kernel(n_rows, n_width, *refs), out_shape=ou...]
    all_gather x3 -> x0, waiting for transfers between devices: 153 us -> none  [the longest x1 130 us: shards(): lax.all_gather(narrow_query, 'rows', axis=0, tiled=True)]
    unnamed x1 -> x0, blocking collectives: 39.8 us -> none
    psum x1 -> x0, blocking collectives: 25.5 us -> none  [shards(): lax.psum((jnp.sum(result_query * result_query, axis=0), jnp.sum(result_ke...]
    unnamed x29 -> x4, local copies, waits for them, and re-layouts: 26.7 us -> 3.87 us
    convert_element_type x3 -> x0, other arithmetic: 9.51 us -> none  [the longest x1 7.05 us: shards(): (result_query / column_query).astype(jnp.bfloat16)]
    reduce_sum x2 -> x0, other arithmetic: 5.92 us -> none  [the longest x1 5.54 us: shards(): jnp.sum(result_query * result_query, axis=0)]
  transfers between devices with their start and end apart: 3 -> 0, of which waited for: 2 -> 0; matrix products, arithmetic and copies ran while one was open for 3% -> 0% of each run, Pallas kernels for 0% -> 0%
where the time goes in v1:
time: 171 us
  Pallas kernels  162 us (95%)
  local copies, waits for them, and re-layouts  6.87 us (4%)
    pallas_call x1, Pallas kernels, shards(): pl.pallas_call(lambda *refs: kernel(n_rows, n_width, *refs), out_shape=ou...  151 us
    pallas_call x1, Pallas kernels, shards(): pl.pallas_call(store, out_shape=(jax.ShapeDtypeStruct((total, wide_query)...  11 us
    unnamed x4, local copies, waits for them, and re-layouts  3.87 us

profile of v1, /device:TPU:0, one launch (start us, length us, event | category | flops | bytes accessed | tf_op | source)
XLA Modules:
  0.0 170.6 jit_solution(13962252585853623677)
XLA Ops:
  0.6 0.7 add.5
  1.3 0.6 pad.4
  1.9 1.6 broadcast_in_dim.2.refs_0_
  3.5 150.8 %shard_map.144 = (bf16[7168,256]{1,0:T(8,128)(2,1)S(1)}, bf16[7168,256]{1,0:T(8,128)(2,1)S(1)}, bf16[7168,256]{1,0:T(8,128)(2,1)S(1)}, bf16[7168,256]{1,0:T(8,12...) custom-call(f32[896,128]{1,0:T(8,128)} %broadcast_in_dim.2.refs_0_, ...), custom_call_target="tpu_custom_call" | custom-call | tf_op jit(solution)/shard_map/pallas_call | solution.py:258
  154.3 0.0 copy-start
  154.3 1.8 %copy-done = bf16[7168,256]{1,0:T(8,128)(2,1)} copy-done((bf16[7168,256]{1,0:T(8,128)(2,1)}, bf16[7168,256]{1,0:T(8,128)(2,1)S(1)}, u32[]{:S(2)}) %copy-start) | copy-done | bytes 3670040
  156.2 0.0 copy-start.1
  156.2 2.0 %copy-done.1 = bf16[7168,256]{1,0:T(8,128)(2,1)S(1)} copy-done((bf16[7168,256]{1,0:T(8,128)(2,1)S(1)}, bf16[7168,256]{1,0:T(8,128)(2,1)}, u32[]{:S(2)}) %copy-start.1) | copy-done | bytes 3670040
  158.2 11.0 %shard_map.145 = (bf16[7168,1792]{1,0:T(8,128)(2,1)}, bf16[7168,256]{1,0:T(8,128)(2,1)}, bf16[7168,256]{1,0:T(8,128)(2,1)}, f32[1,1792]{1,0:T(1,128)S(1)}, f32[1...) custom-call(bf16[7168,256]{1,0:T(8,128)(2,1)S(1)} %get-tuple-element.27.refs_0_, ...), custom_call_target="tpu_custom_call" | custom-call | tf_op jit(solution)/shard_map/pallas_call | solution.py:283
  169.2 0.6 reduce
  169.8 0.1 fusion
  169.9 0.7 convert_element_type.7
Async XLA Ops:
  154.3 1.8 %copy-start = (bf16[7168,256]{1,0:T(8,128)(2,1)}, bf16[7168,256]{1,0:T(8,128)(2,1)S(1)}, u32[]{:S(2)}) copy-start(bf16[7168,256]{1,0:T(8,128)(2,1)S(1)} %get-tuple-element.29.refs_2_) | copy-start | bytes 11010052
  156.2 2.0 %copy-start.1 = (bf16[7168,256]{1,0:T(8,128)(2,1)S(1)}, bf16[7168,256]{1,0:T(8,128)(2,1)}, u32[]{:S(2)}) copy-start(bf16[7168,256]{1,0:T(8,128)(2,1)} %copy-done) | copy-start | bytes 11010052

commit v2 on v1

--- a/solution.py
+++ b/solution.py
@@ -7,13 +7,16 @@
 
 MESH = pl.DeviceIdType.MESH
 LANES = 128
+WINDOW = 4
+EARLY = 2
 
 
 def kernel(
     n_rows,
     n_width,
-    share,
-    norm_in,
+    share_in,
+    norm_train,
+    norm_step,
     one_query,
     other_query,
     one_key,
@@ -23,9 +26,10 @@
     *refs,
 ):
     blocks = refs[: 2 + one_query.shape[1] // one_key.shape[1]]
-    col_query, col_key, col_value, norm_all, first, second, part, in_sem = refs[len(blocks) :][:8]
-    norm_send, norm_recv, slab_send, slab_recv, sum_send, sum_recv = refs[len(blocks) + 8 :][:6]
-    ring_send, ring_recv, twin_send, twin_recv = refs[len(blocks) + 14 :]
+    col_query, col_key, col_value, norm_all, first, second, share = refs[len(blocks) :][:7]
+    part_early, part_late, in_sem, norm_send, norm_recv = refs[len(blocks) + 7 :][:5]
+    slab_send, slab_recv, sum_send, sum_recv = refs[len(blocks) + 12 :][:4]
+    ring_send, ring_recv, twin_send, twin_recv = refs[len(blocks) + 16 :]
     me = lax.axis_index("rows")
     lane = lax.axis_index("width")
     depth, wide = one_key.shape
@@ -43,11 +47,16 @@
     for g, (one, other, _, _, at) in enumerate(groups):
         a = pltpu.make_async_copy(one.at[:, pl.ds(at, wide)], first.at[g], in_sem.at[0, g])
         b = pltpu.make_async_copy(other.at[:, pl.ds(at, wide)], second.at[g], in_sem.at[1, g])
-        a.start()
-        b.start()
         loads.append((a, b))
-
-    norm_all[me, lane] = norm_in[...]
+        if g < WINDOW:
+            a.start()
+            b.start()
+
+    norm_all[me, lane] = (norm_train[...] + norm_step[...]).reshape(1, -1)
+    for at in range(0, depth, LANES):
+        size = min(LANES, depth - at)
+        line = share_in[pl.ds(at, size)].reshape(1, size)
+        share[pl.ds(at, size), :] = jnp.broadcast_to(line, (LANES, size)).T
 
     barrier = pltpu.get_barrier_semaphore()
     for d in range(1, n_rows):
@@ -73,9 +82,26 @@
         copy.start()
         norm_copies.append(copy)
 
+    def send_sums(part, kind):
+        copies = []
+        for d in range(1, n_rows):
+            copy = pltpu.make_async_remote_copy(
+                src_ref=part.at[me],
+                dst_ref=part.at[me],
+                send_sem=sum_send.at[kind, d],
+                recv_sem=sum_recv.at[kind, d],
+                device_id={"rows": lax.rem(me + d, n_rows)},
+                device_id_type=MESH,
+            )
+            copy.start()
+            copies.append(copy)
+        return copies
+
     for g in range(len(groups)):
-        loads[g][0].wait()
-        loads[g][1].wait()
+        for load in loads[g]:
+            load.wait()
+        for load in loads[g + WINDOW] if g + WINDOW < len(groups) else ():
+            load.start()
 
         def mix(i, acc):
             rows = pl.ds(pl.multiple_of(i * tile, tile), tile)
@@ -86,20 +112,15 @@
             return acc + jnp.sum((r * r).reshape(tile // 8, 8, wide), axis=0)
 
         acc = lax.fori_loop(0, depth // tile, mix, jnp.zeros((8, wide), jnp.float32))
-        part[me, g] = jnp.sum(acc, axis=0, keepdims=True)
-
-    sum_copies = []
-    for d in range(1, n_rows):
-        copy = pltpu.make_async_remote_copy(
-            src_ref=part.at[me],
-            dst_ref=part.at[me],
-            send_sem=sum_send.at[d],
-            recv_sem=sum_recv.at[d],
-            device_id={"rows": lax.rem(me + d, n_rows)},
-            device_id_type=MESH,
-        )
-        copy.start()
-        sum_copies.append(copy)
+        line = jnp.sum(acc, axis=0, keepdims=True)
+        if g < EARLY:
+            part_early[me, g] = line
+        else:
+            part_late[me, g - EARLY] = line
+        if g == EARLY:
+            early_copies = send_sums(part_early, 0)
+
+    late_copies = send_sums(part_late, 1)
 
     for copy in norm_copies:
         copy.wait_recv()
@@ -116,9 +137,6 @@
         copy.start()
         slab_copies.append(copy)
 
-    for copy in sum_copies:
-        copy.wait_recv()
-
     core = lax.rem(me, 2)
     chip = me // 2
     chips = n_rows // 2
@@ -171,11 +189,15 @@
 
     flying = {}
     for g, (_, _, out, col, at) in enumerate(groups):
-        total = part[0, g]
+        if g in (0, EARLY):
+            for copy in early_copies if g == 0 else late_copies:
+                copy.wait_recv()
+        part, line = (part_early, g) if g < EARLY else (part_late, g - EARLY)
+        total = part[0, line]
         for p in range(1, n_rows):
-            total = total + part[p, g]
+            total = total + part[p, line]
         scale = jnp.sqrt(total)
-        col[:, pl.ds(at, wide)] = scale
+        col[pl.ds(at, wide)] = scale.reshape(wide)
         inverse = 1.0 / scale
 
         def narrow(i, carry):
@@ -203,7 +225,7 @@
         copy.wait_send()
     for copy in waits:
         copy.wait()
-    for copy in norm_copies + sum_copies:
+    for copy in norm_copies + early_copies + late_copies:
         copy.wait_send()
     for copy in slab_copies:
         copy.wait()
@@ -241,36 +263,35 @@
         wide_query = one_query.shape[1]
         count = 2 + wide_query // wide
         piece = norm_train.shape[0]
-        padded = -(-piece // LANES) * LANES
-        share = jnp.broadcast_to(mix_share[:, None], (depth, LANES))
-        norm = jnp.pad(norm_train + norm_step, (0, padded - piece)).reshape(1, padded)
         total = depth * n_rows
         reach = n_rows // 4
         hbm = pl.BlockSpec(memory_space=pltpu.HBM)
         vmem = pl.BlockSpec(memory_space=pltpu.VMEM)
         dma = pltpu.SemaphoreType.DMA
         out_shape = (pltpu.VMEM((total, wide), jnp.bfloat16),) * count + (
-            pltpu.VMEM((1, wide_query), jnp.float32),
-            pltpu.VMEM((1, wide), jnp.float32),
-            pltpu.VMEM((1, wide), jnp.float32),
-            pltpu.VMEM((n_rows, n_width, 1, padded), jnp.float32),
+            pltpu.VMEM((wide_query,), jnp.float32),
+            pltpu.VMEM((wide,), jnp.float32),
+            pltpu.VMEM((wide,), jnp.float32),
+            pltpu.VMEM((n_rows, n_width, 1, piece), jnp.float32),
         )
         gathered = pl.pallas_call(
             lambda *refs: kernel(n_rows, n_width, *refs),
             out_shape=out_shape,
-            in_specs=[vmem] * 2 + [hbm] * 6,
+            in_specs=[vmem] * 3 + [hbm] * 6,
             out_specs=[vmem] * (count + 4),
             scratch_shapes=[
                 pltpu.VMEM((count, depth, wide), jnp.float32),
                 pltpu.VMEM((count, depth, wide), jnp.float32),
-                pltpu.VMEM((n_rows, count, 1, wide), jnp.float32),
+                pltpu.VMEM((depth, LANES), jnp.float32),
+                pltpu.VMEM((n_rows, EARLY, 1, wide), jnp.float32),
+                pltpu.VMEM((n_rows, count - EARLY, 1, wide), jnp.float32),
                 dma((2, count)),
                 dma((n_width,)),
                 dma((n_width,)),
                 dma((n_rows,)),
                 dma((n_rows,)),
-                dma((n_rows,)),
-                dma((n_rows,)),
+                dma((2, n_rows)),
+                dma((2, n_rows)),
                 dma((2, reach, count)),
                 dma((2, reach, count)),
                 dma((1 + 2 * reach, count)),
@@ -279,7 +300,7 @@
             compiler_params=pltpu.CompilerParams(
                 collective_id=0, has_side_effects=True, vmem_limit_bytes=24 * 1024 * 1024
             ),
-        )(share, norm, one_query, other_query, one_key, other_key, one_value, other_value)
+        )(mix_share, norm_train, norm_step, one_query, other_query, one_key, other_key, one_value, other_value)
         final_query, final_key, final_value, col_query, col_key, col_value, norm_all = pl.pallas_call(
             store,
             out_shape=(
@@ -293,14 +314,14 @@
             scratch_shapes=[dma((count + 4,))],
             compiler_params=pltpu.CompilerParams(vmem_limit_bytes=1024 * 1024),
         )(*gathered)
-        serve_norm = norm_all[..., 0, :piece].astype(jnp.bfloat16).reshape(-1)
+        serve_norm = norm_all[..., 0, :].astype(jnp.bfloat16).reshape(-1)
         return (
             final_query,
             final_key,
             final_value,
-            col_query.reshape(-1),
-            col_key.reshape(-1),
-            col_value.reshape(-1),
+            col_query,
+            col_key,
+            col_value,
             serve_norm,
         )
 

time: 171 us -> 166 us (0.971)
  local copies, waits for them, and re-layouts: 6.87 us -> 4.57 us
where the time goes in v2:
time: 166 us
  Pallas kernels  161 us (97%)
  local copies, waits for them, and re-layouts  4.57 us (3%)
    pallas_call x1, Pallas kernels, shards(): pl.pallas_call(lambda *refs: kernel(n_rows, n_width, *refs), out_shape=ou...  150 us
    pallas_call x1, Pallas kernels, shards(): pl.pallas_call(store, out_shape=(jax.ShapeDtypeStruct((total, wide_query)...  11 us
    unnamed x4, local copies, waits for them, and re-layouts  3.87 us

profile of v2, /device:TPU:0, one launch (start us, length us, event | category | flops | bytes accessed | tf_op | source)
XLA Modules:
  0.0 166.0 jit_solution(9195882393672812812)
XLA Ops:
  0.6 149.6 %shard_map.144 = (bf16[7168,256]{1,0:T(8,128)(2,1)S(1)}, bf16[7168,256]{1,0:T(8,128)(2,1)S(1)}, bf16[7168,256]{1,0:T(8,128)(2,1)S(1)}, bf16[7168,256]{1,0:T(8,12...) custom-call(f32[896]{0:T(1024)} %refs_0_.1, ...), custom_call_target="tpu_custom_call" | custom-call | tf_op jit(solution)/shard_map/pallas_call | solution.py:277
  150.3 0.0 copy-start
  150.3 1.8 %copy-done = bf16[7168,256]{1,0:T(8,128)(2,1)} copy-done((bf16[7168,256]{1,0:T(8,128)(2,1)}, bf16[7168,256]{1,0:T(8,128)(2,1)S(1)}, u32[]{:S(2)}) %copy-start) | copy-done | bytes 3670040
  152.1 0.0 copy-start.1
  152.1 2.0 %copy-done.1 = bf16[7168,256]{1,0:T(8,128)(2,1)S(1)} copy-done((bf16[7168,256]{1,0:T(8,128)(2,1)S(1)}, bf16[7168,256]{1,0:T(8,128)(2,1)}, u32[]{:S(2)}) %copy-start.1) | copy-done | bytes 3670040
  154.2 11.0 %shard_map.145 = (bf16[7168,1792]{1,0:T(8,128)(2,1)}, bf16[7168,256]{1,0:T(8,128)(2,1)}, bf16[7168,256]{1,0:T(8,128)(2,1)}, f32[1792]{0:T(1024)}, f32[256]{0:T(2...) custom-call(bf16[7168,256]{1,0:T(8,128)(2,1)S(1)} %get-tuple-element.27.refs_0_, ...), custom_call_target="tpu_custom_call" | custom-call | tf_op jit(solution)/shard_map/pallas_call | solution.py:304
  165.2 0.1 convert_reduce_fusion
  165.3 0.7 convert_element_type.8
Async XLA Ops:
  150.3 1.8 %copy-start = (bf16[7168,256]{1,0:T(8,128)(2,1)}, bf16[7168,256]{1,0:T(8,128)(2,1)S(1)}, u32[]{:S(2)}) copy-start(bf16[7168,256]{1,0:T(8,128)(2,1)S(1)} %get-tuple-element.29.refs_2_) | copy-start | bytes 11010052
  152.1 2.0 %copy-start.1 = (bf16[7168,256]{1,0:T(8,128)(2,1)S(1)}, bf16[7168,256]{1,0:T(8,128)(2,1)}, u32[]{:S(2)}) copy-start(bf16[7168,256]{1,0:T(8,128)(2,1)} %copy-done) | copy-start | bytes 11010052
